TPU v7x, 32 devices: a whole 2x2x4 slice. The times are simulated.
32 devices in a mesh: level: 4 (over y, core), blk: 8 (over z, x).
Axes of the slice: x: 2, y: 2, z: 4, core: 2. Of those that a mesh axis runs over, the one named last changes fastest.
Arguments:
- right_sides: bfloat16 [4, 8, 1024, 384], P('level', 'blk'), may hold values from -6 to 6
- diag_inverse: bfloat16 [4, 8, 1, 1024, 1024], P('level', 'blk'), may hold values from -0.1875 to 0.1875
- compress_basis: bfloat16 [4, 8, 1024, 256], P('level', 'blk'), may hold values from -0.1875 to 0.1875
- expand_basis: bfloat16 [4, 8, 1024, 256], P('level', 'blk'), may hold values from -0.125 to 0.125
- target_ranks: int32 [4, 8], P('level', 'blk'), may hold values from 32 to 256
- coupling: int32 [4, 8, 4, 8], replicated, may hold values 0 or 1
- section_order: int32 [4], replicated, may hold values from 0 to 3, each once
Outputs:
- solved: bfloat16 [4, 8, 1024, 384], P('level', 'blk')
All inputs are finite; a program needn't handle non-finite values.
Results may differ from a plain program's by a relative error of at most 0.015.
Values may be sent and summed in bfloat16 or wider, within the bound.
No kernel may reach another device: no remote copies, remote signals or barrier semaphores. Data moves between devices by JAX's collectives and lax.ppermute only.
A program may use at most 128 MiB of HBM per device.

v0:
```python
import jax
import jax.numpy as jnp
from jax import lax
from jax.sharding import PartitionSpec as P


def per_device(
    right_sides, diag_inverse, compress_basis, expand_basis, target_ranks, coupling, section_order
):
    levels = lax.axis_size("level")
    blocks = lax.axis_size("blk")
    my_level = lax.axis_index("level")
    my_block = lax.axis_index("blk")
    sides_here = right_sides[0, 0]
    inverse_here = diag_inverse[0, 0]
    basis_here = compress_basis[0, 0]
    expand_here = expand_basis[0, 0]
    rank_cap = basis_here.shape[1]
    seg_rows = sides_here.shape[0]
    sub_blocks = inverse_here.shape[0]
    block_rows = inverse_here.shape[1]
    kept_rows = (jnp.arange(rank_cap, dtype=jnp.int32) < target_ranks[0, 0])[:, None]
    my_section = section_order[my_level]
    level_ids = jnp.arange(levels, dtype=jnp.int32)

    def solve(incoming, columns):
        update = jnp.dot(
            expand_here, incoming.astype(jnp.bfloat16), preferred_element_type=jnp.float32
        )
        work_rows = (columns.astype(jnp.float32) - update).astype(jnp.bfloat16)
        work_rows = work_rows.reshape(sub_blocks, block_rows, columns.shape[1])
        solved_rows = jnp.einsum(
            "jab,jbr->jar", inverse_here, work_rows, preferred_element_type=jnp.float32
        )
        solved_rows = solved_rows.astype(jnp.bfloat16).reshape(seg_rows, columns.shape[1])
        coef_rows = lax.dot_general(
            basis_here, solved_rows, (((0,), (0,)), ((), ())), preferred_element_type=jnp.float32
        )
        coef_rows = jnp.where(kept_rows, coef_rows, 0.0).astype(jnp.bfloat16)
        return (solved_rows, coef_rows)

    def advance(carry_state, level_step, columns):
        incoming, solved_rows, coef_rows = carry_state
        solved_rows, coef_rows = lax.cond(
            my_section == level_step,
            lambda: solve(incoming, columns),
            lambda: (solved_rows, coef_rows),
        )
        if level_step == levels - 1:
            return (incoming, solved_rows, coef_rows)
        root_level = jnp.sum(jnp.where(section_order == level_step, level_ids, 0))
        is_later = (my_section > level_step).astype(jnp.float32)
        width_now = columns.shape[1]
        masked = jnp.where(my_level == root_level, coef_rows.astype(jnp.float32), 0.0)
        share = lax.psum_scatter(
            masked.astype(jnp.bfloat16), "level", scatter_dimension=1, tiled=True
        )
        share_cols = share.shape[1]
        gathered = lax.all_gather(share[None], "blk", axis=0, tiled=True)
        dest_weights = coupling[:, my_block, root_level, :].astype(jnp.bfloat16)
        sums = jnp.dot(
            dest_weights, gathered.reshape(blocks, -1), preferred_element_type=jnp.float32
        )
        sums = sums.reshape(levels, rank_cap, share_cols)
        arrived = lax.all_to_all(sums, "level", split_axis=0, concat_axis=2, tiled=True)
        arrived = arrived.reshape(rank_cap, width_now)
        return (incoming + is_later * arrived, solved_rows, coef_rows)

    width_now = sides_here.shape[1]
    carry_state = (
        jnp.zeros((rank_cap, width_now), jnp.float32),
        jnp.zeros((seg_rows, width_now), jnp.bfloat16),
        jnp.zeros((rank_cap, width_now), jnp.bfloat16),
    )
    for level_step in range(levels):
        carry_state = advance(carry_state, level_step, sides_here)
    result = carry_state[1]
    return result[None, None]


def solution(mesh):
    return jax.shard_map(
        per_device,
        mesh=mesh,
        in_specs=(
            P("level", "blk", None, None),
            P("level", "blk", None, None, None),
            P("level", "blk", None, None),
            P("level", "blk", None, None),
            P("level", "blk"),
            P(),
            P(),
        ),
        out_specs=P("level", "blk", None, None),
        check_vma=False,
    )
```

profile of v0, /device:TPU:1, one launch (start us, length us, event | category | flops | bytes accessed | tf_op | source)
XLA Modules:
  0.0 240.1 jit_solution(6065074242285254970)
XLA Ops:
  6.5 1.5 fusion.52
  8.0 1.3 dynamic_slice.12
  10.0 1.4 copy.24
  12.8 1.0 conditional.4
  12.8 1.0 broadcast_in_dim.52
  13.8 0.7 select_convert_fusion.2
  20.5 0.8 dynamic-slice_convert_fusion
  21.4 18.5 %reduce-scatter.4.cloned.1.call-done = bf16[256,96]{0,1:T(8,128)(2,1)} async-done(((bf16[256,384]{0,1:T(8,128)(2,1)}), bf16[256,96]{0,1:T(8,128)(2,1)}) %reduce-scatter.4.cloned.1.call-update) | async-done | bytes 49168 | tf_op jit(solution)/shard_map/reduce_scatter | solution.py:55
  39.9 25.3 %all-gather = bf16[2048,96]{0,1:T(8,128)(2,1)S(1)} all-gather(bf16[256,96]{0,1:T(8,128)(2,1)} %reduce-scatter.4.cloned.1.call-done), channel_id=2, replica_groups=mesh['level'=4,'blk'=8] {'blk'}, dimensions={0}, use_global_device_ids=true | all-gather | bytes 442368 | tf_op jit(solution)/shard_map/all_gather | solution.py:59
  65.5 0.7 reshape.110
  67.4 0.8 copy.27
  68.2 10.6 %all-to-all-start = ((f32[4,256,96]{1,2,0:T(8,128)}), f32[4,256,96]{1,2,0:T(8,128)S(1)}, u32[]{:S(2)}, u32[]{:S(2)}) async-start(f32[4,256,96]{1,2,0:T(8,128)} %copy.27), calls=%async_computation.1 | async-start | bytes 786432 | tf_op jit(solution)/shard_map/all_to_all | solution.py:65
  80.7 4.5 %all-to-all-done = f32[4,256,96]{1,2,0:T(8,128)S(1)} async-done(((f32[4,256,96]{1,2,0:T(8,128)}), f32[4,256,96]{1,2,0:T(8,128)S(1)}, u32[]{:S(2)}, u32[]{:S(2)}) %all-to-all-start) | async-done | bytes 393248 | tf_op jit(solution)/shard_map/all_to_all | solution.py:65
  85.2 0.7 select_convert_fusion.1
  86.0 25.5 %reduce-scatter.6.cloned.1.call-done = bf16[256,96]{0,1:T(8,128)(2,1)} async-done(((bf16[256,384]{0,1:T(8,128)(2,1)}), bf16[256,96]{0,1:T(8,128)(2,1)}) %reduce-scatter.6.cloned.1.call-update) | async-done | bytes 49168 | tf_op jit(solution)/shard_map/reduce_scatter | solution.py:55
  111.5 25.3 %all-gather.1 = bf16[2048,96]{0,1:T(8,128)(2,1)S(1)} all-gather(bf16[256,96]{0,1:T(8,128)(2,1)} %reduce-scatter.6.cloned.1.call-done), channel_id=3, replica_groups=mesh['level'=4,'blk'=8] {'blk'}, dimensions={0}, use_global_device_ids=true | all-gather | bytes 442368 | tf_op jit(solution)/shard_map/all_gather | solution.py:59
  137.1 0.7 reshape.111
  137.8 0.5 dot_general.62
  138.9 0.8 copy.32
  139.8 10.7 %all-to-all-start.1 = ((f32[4,256,96]{1,2,0:T(8,128)}), f32[4,256,96]{1,2,0:T(8,128)S(1)}, u32[]{:S(2)}, u32[]{:S(2)}) async-start(f32[4,256,96]{1,2,0:T(8,128)} %copy.32), calls=%async_computation.3 | async-start | bytes 786432 | tf_op jit(solution)/shard_map/all_to_all | solution.py:65
  152.5 4.4 %all-to-all-done.1 = f32[4,256,96]{1,2,0:T(8,128)S(1)} async-done(((f32[4,256,96]{1,2,0:T(8,128)}), f32[4,256,96]{1,2,0:T(8,128)S(1)}, u32[]{:S(2)}, u32[]{:S(2)}) %all-to-all-start.1) | async-done | bytes 393248 | tf_op jit(solution)/shard_map/all_to_all | solution.py:65
  157.0 0.7 select_convert_fusion
  157.7 25.5 %reduce-scatter.8.cloned.1.call-done = bf16[256,96]{0,1:T(8,128)(2,1)} async-done(((bf16[256,384]{0,1:T(8,128)(2,1)}), bf16[256,96]{0,1:T(8,128)(2,1)}) %reduce-scatter.8.cloned.1.call-update) | async-done | bytes 49168 | tf_op jit(solution)/shard_map/reduce_scatter | solution.py:55
  183.3 25.5 %all-gather.2 = bf16[2048,96]{0,1:T(8,128)(2,1)S(1)} all-gather(bf16[256,96]{0,1:T(8,128)(2,1)} %reduce-scatter.8.cloned.1.call-done), channel_id=4, replica_groups=mesh['level'=4,'blk'=8] {'blk'}, dimensions={0}, use_global_device_ids=true | all-gather | bytes 442368 | tf_op jit(solution)/shard_map/all_gather | solution.py:59
  209.1 0.7 reshape.112
  209.8 0.5 dot_general.65
  211.0 0.8 copy.37
  211.8 10.5 %all-to-all-start.2 = ((f32[4,256,96]{1,2,0:T(8,128)}), f32[4,256,96]{1,2,0:T(8,128)S(1)}, u32[]{:S(2)}, u32[]{:S(2)}) async-start(f32[4,256,96]{1,2,0:T(8,128)} %copy.37), calls=%async_computation.5 | async-start | bytes 786432 | tf_op jit(solution)/shard_map/all_to_all | solution.py:65
  223.0 5.8 %all-to-all-done.2 = f32[4,256,96]{1,2,0:T(8,128)S(1)} async-done(((f32[4,256,96]{1,2,0:T(8,128)}), f32[4,256,96]{1,2,0:T(8,128)S(1)}, u32[]{:S(2)}, u32[]{:S(2)}) %all-to-all-start.2) | async-done | bytes 393248 | tf_op jit(solution)/shard_map/all_to_all | solution.py:65
  228.8 3.9 %conditional.7 = (bf16[1,1,1024,384]{3,2,1,0:T(8,128)(2,1)S(1)}) conditional(s32[]{:T(128)} %bitcast.17, bf16[1024,384]{0,1:T(8,128)(2,1)} %get-tuple-element.110, (bf16[1024,384]{0,1:T(8,128)(2,1)S(1)}, s32[1]{0:T(128)}, f32[1,256,4,96]{1,3,2,0:T(8,128)S(1)}, f32[256,384]{0,1:T(8,128)S(1)}, bf16[1024,256]{1,0:T(8,128)(2,1)S(1)}, ...), branch_computations={%region_12.13_spmd, %region_13.14_spmd} | conditional | flops 1008500736 | bytes 7733274 | solution.py:44
  229.5 2.8 %fusion.6 = bf16[1,1,1024,384]{2,3,1,0:T(8,128)(2,1)S(1)} fusion(bf16[1,1024,1024]{2,1,0:T(8,128)(2,1)} %get-tuple-element.103, bf16[1024,384]{0,1:T(8,128)(2,1)S(1)} %get-tuple-element.98, bf16[256,384]{0,1:T(8,128)(2,1)S(1)} %fusion.9, bf16[1024,256]{1,0:T(8,128)(2,1)S(1)} %get-tuple-element.102), kind=kOutput, calls=%fused_computation.5 | convolution fusion | flops 1008205824 | bytes 4390912 | tf_op jit(solution)/shard_map/cond/branch_1_fun/jab,jbr->jar/dot_general | solution.py:32
  232.7 0.9 copy-done
  (35 shorter events, 3.8 us)
Async XLA Ops:
  6.5 6.2 %copy-start.2 = (bf16[1,1,1024,256]{3,2,1,0:T(8,128)(2,1)S(1)}, bf16[1,1,1024,256]{3,2,1,0:T(8,128)(2,1)}, u32[]{:S(2)}) copy-start(bf16[1,1,1024,256]{3,2,1,0:T(8,128)(2,1)} %param.18) | copy-start | bytes 1572868
  6.5 6.2 %copy-start.1 = (bf16[1,1,1024,256]{3,2,1,0:T(8,128)(2,1)S(1)}, bf16[1,1,1024,256]{3,2,1,0:T(8,128)(2,1)}, u32[]{:S(2)}) copy-start(bf16[1,1,1024,256]{3,2,1,0:T(8,128)(2,1)} %param.17) | copy-start | bytes 1572868
  6.5 33.3 %reduce-scatter.4.cloned.1.call-start = ((), (), s32[]{:S(2)}) async-start(), calls=%async_computation.6 | async-start | bytes 245760 | tf_op jit(solution)/shard_map/reduce_scatter | solution.py:55
  68.2 17.0 %all-to-all-start = ((f32[4,256,96]{1,2,0:T(8,128)}), f32[4,256,96]{1,2,0:T(8,128)S(1)}, u32[]{:S(2)}, u32[]{:S(2)}) async-start(f32[4,256,96]{1,2,0:T(8,128)} %copy.27), calls=%async_computation.1 | async-start | bytes 786432 | tf_op jit(solution)/shard_map/all_to_all | solution.py:65
  78.8 32.7 %reduce-scatter.6.cloned.1.call-start = ((), (), s32[]{:S(2)}) async-start(), calls=%async_computation.7 | async-start | bytes 245760 | tf_op jit(solution)/shard_map/reduce_scatter | solution.py:55
  139.8 17.2 %copy-start.3 = (bf16[1,1,1024,256]{3,2,1,0:T(8,128)(2,1)S(1)}, bf16[1,1,1024,256]{3,2,1,0:T(8,128)(2,1)}, u32[]{:S(2)}) copy-start(bf16[1,1,1024,256]{3,2,1,0:T(8,128)(2,1)} %param.18) | copy-start | bytes 1572868
  139.8 17.1 %all-to-all-start.1 = ((f32[4,256,96]{1,2,0:T(8,128)}), f32[4,256,96]{1,2,0:T(8,128)S(1)}, u32[]{:S(2)}, u32[]{:S(2)}) async-start(f32[4,256,96]{1,2,0:T(8,128)} %copy.32), calls=%async_computation.3 | async-start | bytes 786432 | tf_op jit(solution)/shard_map/all_to_all | solution.py:65
  150.5 32.8 %reduce-scatter.8.cloned.1.call-start = ((), (), s32[]{:S(2)}) async-start(), calls=%async_computation.8 | async-start | bytes 245760 | tf_op jit(solution)/shard_map/reduce_scatter | solution.py:55
  210.4 18.4 %copy-start.4 = (bf16[1,1,1024,256]{3,2,1,0:T(8,128)(2,1)S(1)}, bf16[1,1,1024,256]{3,2,1,0:T(8,128)(2,1)}, u32[]{:S(2)}) copy-start(bf16[1,1,1024,256]{3,2,1,0:T(8,128)(2,1)} %param.18) | copy-start | bytes 1572868
  211.8 17.0 %all-to-all-start.2 = ((f32[4,256,96]{1,2,0:T(8,128)}), f32[4,256,96]{1,2,0:T(8,128)S(1)}, u32[]{:S(2)}, u32[]{:S(2)}) async-start(f32[4,256,96]{1,2,0:T(8,128)} %copy.37), calls=%async_computation.5 | async-start | bytes 786432 | tf_op jit(solution)/shard_map/all_to_all | solution.py:65
  232.7 0.9 copy-start
Sparse Core Ops, SparseCore 0:
  14.6 25.2 reduce-scatter.3
  86.1 25.3 reduce-scatter.5
  157.9 25.3 reduce-scatter.7
where the time goes:
time: 241 us; the launch traced here: 240 us
  waiting for transfers between devices  84.2 us (35%)
  blocking collectives  76.2 us (32%)
  starting transfers between devices  31.8 us (13%)
  between operations  26 us (11%)
  local copies, waits for them, and re-layouts  13 us (5%)
  other arithmetic  4.62 us (2%)
  matrix products  3.55 us (1%)
    all_gather x3, blocking collectives, advance(): gathered = lax.all_gather(share[None], 'blk', axis=0, tiled=True)  76.2 us
    reduce_scatter x3, waiting for transfers between devices, advance(): lax.psum_scatter(masked.astype(jnp.bfloat16), 'level', scatter_dimension=...  69.5 us
    all_to_all x3, starting transfers between devices, advance(): lax.all_to_all(sums, 'level', split_axis=0, concat_axis=2, tiled=True)  31.8 us
    all_to_all x3, waiting for transfers between devices, advance(): lax.all_to_all(sums, 'level', split_axis=0, concat_axis=2, tiled=True)  14.6 us
    dot_general x9, local copies, waits for them, and re-layouts, advance(): jnp.dot(dest_weights, gathered.reshape(blocks, -1), preferred_element_typ...  5.09 us
  transfers between devices with their start and end apart: 6, of which 6 were waited for; matrix products, arithmetic and copies ran while one was open for 0% of the time, Pallas kernels for 0%

commit v1 on v0

--- a/solution.py
+++ b/solution.py
@@ -62,7 +62,12 @@
             dest_weights, gathered.reshape(blocks, -1), preferred_element_type=jnp.float32
         )
         sums = sums.reshape(levels, rank_cap, share_cols)
-        arrived = lax.all_to_all(sums, "level", split_axis=0, concat_axis=2, tiled=True)
+        arrived = jnp.concatenate(
+            lax.all_to_all(
+                jnp.stack(jnp.split(sums, lax.axis_size("level"), axis=0)), "level", 0, 0
+            ),
+            axis=2,
+        )
         arrived = arrived.reshape(rank_cap, width_now)
         return (incoming + is_later * arrived, solved_rows, coef_rows)
 

time: 241 us -> 243 us (level)
    dot_general x9 -> x0, local copies, waits for them, and re-layouts: 5.09 us -> none  [advance(): jnp.dot(dest_weights, gathered.reshape(blocks, -1), preferred_element_typ...]
    another operation x0 -> x15, local copies, waits for them, and re-layouts: none -> 3.88 us  [advance(): jnp.stack(jnp.split(sums, lax.axis_size('level'), axis=0))]
    split x0 -> x3, local copies, waits for them, and re-layouts: none -> 3.27 us  [advance(): jnp.split(sums, lax.axis_size('level'), axis=0)]
where the time goes in v1:
time: 243 us; the launch traced here: 242 us
  waiting for transfers between devices  84.6 us (35%)
  blocking collectives  75.9 us (31%)
  starting transfers between devices  31.9 us (13%)
  between operations  25.5 us (10%)
  local copies, waits for them, and re-layouts  15.1 us (6%)
  other arithmetic  4.76 us (2%)
  matrix products  3.56 us (1%)
    all_gather x3, blocking collectives, advance(): gathered = lax.all_gather(share[None], 'blk', axis=0, tiled=True)  75.9 us
    reduce_scatter x3, waiting for transfers between devices, advance(): lax.psum_scatter(masked.astype(jnp.bfloat16), 'level', scatter_dimension=...  69.7 us
    all_to_all x3, starting transfers between devices, advance(): lax.all_to_all(jnp.stack(jnp.split(sums, lax.axis_size('level'), axis=0))...  31.9 us
    all_to_all x3, waiting for transfers between devices, advance(): lax.all_to_all(jnp.stack(jnp.split(sums, lax.axis_size('level'), axis=0))...  14.9 us
  transfers between devices with their start and end apart: 6, of which 6 were waited for; matrix products, arithmetic and copies ran while one was open for 0% of the time, Pallas kernels for 0%

profile of v1, /device:TPU:1, one launch (start us, length us, event | category | flops | bytes accessed | tf_op | source)
XLA Modules:
  0.0 242.3 jit_solution(7633553309865791386)
XLA Ops:
  6.5 1.5 fusion.52
  8.0 1.3 dynamic_slice.12
  10.0 1.4 copy.26
  12.7 1.0 conditional.4
  12.7 1.0 broadcast_in_dim.52
  13.7 0.7 select_convert_fusion.2
  20.3 0.8 dynamic-slice_convert_fusion
  21.1 18.7 %reduce-scatter.4.cloned.1.call-done = bf16[256,96]{0,1:T(8,128)(2,1)} async-done(((bf16[256,384]{0,1:T(8,128)(2,1)}), bf16[256,96]{0,1:T(8,128)(2,1)}) %reduce-scatter.4.cloned.1.call-update) | async-done | bytes 49168 | tf_op jit(solution)/shard_map/reduce_scatter | solution.py:55
  39.8 25.3 %all-gather = bf16[2048,96]{0,1:T(8,128)(2,1)S(1)} all-gather(bf16[256,96]{0,1:T(8,128)(2,1)} %reduce-scatter.4.cloned.1.call-done), channel_id=2, replica_groups=mesh['level'=4,'blk'=8] {'blk'}, dimensions={0}, use_global_device_ids=true | all-gather | bytes 442368 | tf_op jit(solution)/shard_map/all_gather | solution.py:59
  65.4 0.7 reshape.125
  66.4 1.1 slice_reduce_fusion.11
  68.0 0.9 copy.28
  68.9 10.6 %all-to-all-start = ((f32[4,1,256,96]{2,3,1,0:T(8,128)}), f32[4,1,256,96]{2,3,1,0:T(8,128)S(1)}, u32[]{:S(2)}, u32[]{:S(2)}) async-start(f32[4,1,256,96]{2,3,1,0:T(8,128)} %copy.28), calls=%async_computation.1 | async-start | bytes 786432 | tf_op jit(solution)/shard_map/all_to_all | solution.py:66
  81.4 4.5 %all-to-all-done = f32[4,1,256,96]{2,3,1,0:T(8,128)S(1)} async-done(((f32[4,1,256,96]{2,3,1,0:T(8,128)}), f32[4,1,256,96]{2,3,1,0:T(8,128)S(1)}, u32[]{:S(2)}, u32[]{:S(2)}) %all-to-all-start) | async-done | bytes 393248 | tf_op jit(solution)/shard_map/all_to_all | solution.py:66
  86.7 25.5 %reduce-scatter.6.cloned.1.call-done = bf16[256,96]{0,1:T(8,128)(2,1)} async-done(((bf16[256,384]{0,1:T(8,128)(2,1)}), bf16[256,96]{0,1:T(8,128)(2,1)}) %reduce-scatter.6.cloned.1.call-update) | async-done | bytes 49168 | tf_op jit(solution)/shard_map/reduce_scatter | solution.py:55
  112.2 25.3 %all-gather.1 = bf16[2048,96]{0,1:T(8,128)(2,1)S(1)} all-gather(bf16[256,96]{0,1:T(8,128)(2,1)} %reduce-scatter.6.cloned.1.call-done), channel_id=3, replica_groups=mesh['level'=4,'blk'=8] {'blk'}, dimensions={0}, use_global_device_ids=true | all-gather | bytes 442368 | tf_op jit(solution)/shard_map/all_gather | solution.py:59
  137.8 0.7 reshape.126
  138.8 1.1 slice_reduce_fusion.7
  140.3 0.9 copy.33
  141.2 10.7 %all-to-all-start.1 = ((f32[4,1,256,96]{2,3,1,0:T(8,128)}), f32[4,1,256,96]{2,3,1,0:T(8,128)S(1)}, u32[]{:S(2)}, u32[]{:S(2)}) async-start(f32[4,1,256,96]{2,3,1,0:T(8,128)} %copy.33), calls=%async_computation.3 | async-start | bytes 786432 | tf_op jit(solution)/shard_map/all_to_all | solution.py:66
  153.8 4.6 %all-to-all-done.1 = f32[4,1,256,96]{2,3,1,0:T(8,128)S(1)} async-done(((f32[4,1,256,96]{2,3,1,0:T(8,128)}), f32[4,1,256,96]{2,3,1,0:T(8,128)S(1)}, u32[]{:S(2)}, u32[]{:S(2)}) %all-to-all-start.1) | async-done | bytes 393248 | tf_op jit(solution)/shard_map/all_to_all | solution.py:66
  158.6 0.7 select_convert_fusion
  159.4 25.5 %reduce-scatter.8.cloned.1.call-done = bf16[256,96]{0,1:T(8,128)(2,1)} async-done(((bf16[256,384]{0,1:T(8,128)(2,1)}), bf16[256,96]{0,1:T(8,128)(2,1)}) %reduce-scatter.8.cloned.1.call-update) | async-done | bytes 49168 | tf_op jit(solution)/shard_map/reduce_scatter | solution.py:55
  184.9 25.3 %all-gather.2 = bf16[2048,96]{0,1:T(8,128)(2,1)S(1)} all-gather(bf16[256,96]{0,1:T(8,128)(2,1)} %reduce-scatter.8.cloned.1.call-done), channel_id=4, replica_groups=mesh['level'=4,'blk'=8] {'blk'}, dimensions={0}, use_global_device_ids=true | all-gather | bytes 442368 | tf_op jit(solution)/shard_map/all_gather | solution.py:59
  210.4 0.7 reshape.127
  211.4 1.1 slice_reduce_fusion.3
  212.9 0.9 copy.38
  213.9 10.6 %all-to-all-start.2 = ((f32[4,1,256,96]{2,3,1,0:T(8,128)}), f32[4,1,256,96]{2,3,1,0:T(8,128)S(1)}, u32[]{:S(2)}, u32[]{:S(2)}) async-start(f32[4,1,256,96]{2,3,1,0:T(8,128)} %copy.38), calls=%async_computation.5 | async-start | bytes 786432 | tf_op jit(solution)/shard_map/all_to_all | solution.py:66
  225.1 5.8 %all-to-all-done.2 = f32[4,1,256,96]{2,3,1,0:T(8,128)S(1)} async-done(((f32[4,1,256,96]{2,3,1,0:T(8,128)}), f32[4,1,256,96]{2,3,1,0:T(8,128)S(1)}, u32[]{:S(2)}, u32[]{:S(2)}) %all-to-all-start.2) | async-done | bytes 393248 | tf_op jit(solution)/shard_map/all_to_all | solution.py:66
  230.9 3.9 %conditional.7 = (bf16[1,1,1024,384]{3,2,1,0:T(8,128)(2,1)S(1)}) conditional(s32[]{:T(128)} %bitcast.18, bf16[1024,384]{0,1:T(8,128)(2,1)} %get-tuple-element.110, (bf16[1024,384]{0,1:T(8,128)(2,1)S(1)}, s32[1]{0:T(128)}, f32[1,256,4,96]{1,3,0,2:T(8,128)S(1)}, f32[256,384]{0,1:T(8,128)S(1)}, bf16[1024,256]{1,0:T(8,128)(2,1)S(1)}, ...), branch_computations={%region_12.13_spmd, %region_13.14_spmd} | conditional | flops 1008500736 | bytes 7733274 | solution.py:44
  231.7 2.8 %fusion.6 = bf16[1,1,1024,384]{2,3,1,0:T(8,128)(2,1)S(1)} fusion(bf16[1,1024,1024]{2,1,0:T(8,128)(2,1)} %get-tuple-element.103, bf16[1024,384]{0,1:T(8,128)(2,1)S(1)} %get-tuple-element.98, bf16[256,384]{0,1:T(8,128)(2,1)S(1)} %fusion.9, bf16[1024,256]{1,0:T(8,128)(2,1)S(1)} %get-tuple-element.102), kind=kOutput, calls=%fused_computation.5 | convolution fusion | flops 1008205824 | bytes 4390912 | tf_op jit(solution)/shard_map/cond/branch_1_fun/jab,jbr->jar/dot_general | solution.py:32
  234.9 0.9 copy-done
  (47 shorter events, 4.3 us)
Async XLA Ops:
  6.5 6.1 %copy-start.2 = (bf16[1,1,1024,256]{3,2,1,0:T(8,128)(2,1)S(1)}, bf16[1,1,1024,256]{3,2,1,0:T(8,128)(2,1)}, u32[]{:S(2)}) copy-start(bf16[1,1,1024,256]{3,2,1,0:T(8,128)(2,1)} %param.18) | copy-start | bytes 1572868
  6.5 6.2 %copy-start.1 = (bf16[1,1,1024,256]{3,2,1,0:T(8,128)(2,1)S(1)}, bf16[1,1,1024,256]{3,2,1,0:T(8,128)(2,1)}, u32[]{:S(2)}) copy-start(bf16[1,1,1024,256]{3,2,1,0:T(8,128)(2,1)} %param.17) | copy-start | bytes 1572868
  6.5 33.3 %reduce-scatter.4.cloned.1.call-start = ((), (), s32[]{:S(2)}) async-start(), calls=%async_computation.6 | async-start | bytes 245760 | tf_op jit(solution)/shard_map/reduce_scatter | solution.py:55
  68.9 17.0 %all-to-all-start = ((f32[4,1,256,96]{2,3,1,0:T(8,128)}), f32[4,1,256,96]{2,3,1,0:T(8,128)S(1)}, u32[]{:S(2)}, u32[]{:S(2)}) async-start(f32[4,1,256,96]{2,3,1,0:T(8,128)} %copy.28), calls=%async_computation.1 | async-start | bytes 786432 | tf_op jit(solution)/shard_map/all_to_all | solution.py:66
  79.5 32.7 %reduce-scatter.6.cloned.1.call-start = ((), (), s32[]{:S(2)}) async-start(), calls=%async_computation.7 | async-start | bytes 245760 | tf_op jit(solution)/shard_map/reduce_scatter | solution.py:55
  141.2 17.2 %copy-start.3 = (bf16[1,1,1024,256]{3,2,1,0:T(8,128)(2,1)S(1)}, bf16[1,1,1024,256]{3,2,1,0:T(8,128)(2,1)}, u32[]{:S(2)}) copy-start(bf16[1,1,1024,256]{3,2,1,0:T(8,128)(2,1)} %param.18) | copy-start | bytes 1572868
  141.2 17.1 %all-to-all-start.1 = ((f32[4,1,256,96]{2,3,1,0:T(8,128)}), f32[4,1,256,96]{2,3,1,0:T(8,128)S(1)}, u32[]{:S(2)}, u32[]{:S(2)}) async-start(f32[4,1,256,96]{2,3,1,0:T(8,128)} %copy.33), calls=%async_computation.3 | async-start | bytes 786432 | tf_op jit(solution)/shard_map/all_to_all | solution.py:66
  151.9 33.0 %reduce-scatter.8.cloned.1.call-start = ((), (), s32[]{:S(2)}) async-start(), calls=%async_computation.8 | async-start | bytes 245760 | tf_op jit(solution)/shard_map/reduce_scatter | solution.py:55
  212.7 18.3 %copy-start.4 = (bf16[1,1,1024,256]{3,2,1,0:T(8,128)(2,1)S(1)}, bf16[1,1,1024,256]{3,2,1,0:T(8,128)(2,1)}, u32[]{:S(2)}) copy-start(bf16[1,1,1024,256]{3,2,1,0:T(8,128)(2,1)} %param.18) | copy-start | bytes 1572868
  213.9 17.1 %all-to-all-start.2 = ((f32[4,1,256,96]{2,3,1,0:T(8,128)}), f32[4,1,256,96]{2,3,1,0:T(8,128)S(1)}, u32[]{:S(2)}, u32[]{:S(2)}) async-start(f32[4,1,256,96]{2,3,1,0:T(8,128)} %copy.38), calls=%async_computation.5 | async-start | bytes 786432 | tf_op jit(solution)/shard_map/all_to_all | solution.py:66
  234.8 0.9 copy-start
Sparse Core Ops, SparseCore 0:
  14.6 25.2 reduce-scatter.3
  86.8 25.3 reduce-scatter.5
  159.5 25.3 reduce-scatter.7
